TPU v7x, 128 devices: a whole 4x4x4 slice. The times are simulated.
128 devices in a mesh: dp: 16 (over y, x_lo, core), tensor: 8 (over z, x_hi).
Axes of the slice: x: 4 (x_hi: 2, x_lo: 2; x = x_hi * 2 + x_lo), y: 4, z: 4, core: 2. Of those that a mesh axis runs over, the one named last changes fastest.
Arguments:
- arrived: bfloat16 [256, 128, 1536], P(('dp', 'tensor')), may hold values from -6 to 6
- destination: int32 [256], replicated, may hold values from 0 to 15, as said below
- query_of: int32 [256], replicated, may hold values from 0 to 31, as said below
- lengths: int32 [256], replicated, may hold values from 32 to 128
- attn_gain: float32 [1536], replicated, may hold values from 0.25 to 1.75
- q_weight: bfloat16 [1536, 1024], P(None, 'tensor')
- q_bias: bfloat16 [1024], P('tensor'), may hold values from -3 to 3
- k_weight: bfloat16 [1536, 256], replicated
- v_weight: bfloat16 [1536, 256], replicated, may hold values from -0.15625 to 0.15625
- v_bias: bfloat16 [256], replicated, may hold values from -3 to 3
- o_weight: bfloat16 [1024, 1536], P('tensor'), may hold values from -0.1875 to 0.1875
- mlp_gain: float32 [1536], replicated, may hold values from 0.25 to 1.75
- w_gate: bfloat16 [1536, 8960], P(None, 'tensor'), may hold values from -0.15625 to 0.15625
- w_up: bfloat16 [1536, 8960], P(None, 'tensor'), may hold values from -0.15625 to 0.15625
- w_down: bfloat16 [8960, 1536], P('tensor'), may hold values from -0.0625 to 0.0625
- final_gain: float32 [1536], replicated, may hold values from 0.25 to 1.75
- score_weight: float32 [1536], replicated, may hold values from -0.15625 to 0.15625
Outputs:
- hidden_out: bfloat16 [128, 256, 1536], P('tensor', 'dp')
- centred: float32 [256], P('dp')
- query_mean: float32 [32], P('dp')
Inputs may be any that keep to these rules, and one draw needn't show every extreme that they name: In each aligned block of 16 pairs every destination occurs exactly once. `query_of`: each query has exactly 8 pairs.
All inputs are finite; a program needn't handle non-finite values.
Results may differ from a plain program's by a relative error of at most 0.02.
The roundings to bfloat16 on the way count: a program that leaves them out, or rounds other values in their place, can miss the bound.
Values may be sent and summed in bfloat16 or wider, within the bound.
A program may use at most 128 MiB of HBM per device.

v0:
```python
import math
import jax
import jax.numpy as jnp
from jax import lax
from jax.sharding import Mesh
from jax.sharding import PartitionSpec as P

KV_HEADS = 2
HEAD_DIM = 128
HEADS = 8
QUERY_DP = 2
TENSOR = ("tensor_0", "tensor_1")
DP_TENSOR = ("dp", "tensor_0", "tensor_1")
theta_base = 1000000.0
norm_eps = 1e-06


def gather_axes(x, axes, dim):
    for axis in reversed(axes):
        x = lax.all_gather(x, axis, axis=dim, tiled=True)
    return x


def copy_for_each(x, axis):
    copies = jnp.broadcast_to(x, (lax.axis_size(axis), *x.shape))
    return lax.all_to_all(copies, axis, split_axis=0, concat_axis=0, tiled=True)


def taken_together(x, axis):
    return copy_for_each(x, axis).sum(axis=0)


def rms_scale(values, gain_vector):
    floats = values.astype(jnp.float32)
    return (
        floats
        * lax.rsqrt(jnp.mean(floats * floats, axis=-1, keepdims=True) + norm_eps)
        * gain_vector
    )


def frequency_table(head_dim):
    return theta_base ** (-2.0 * jnp.arange(head_dim // 2, dtype=jnp.float32) / head_dim)


def rotate(values, cosine_table, sine_table):
    half_dim = values.shape[-1] // 2
    first_half = values[..., :half_dim]
    second_half = values[..., half_dim:]
    return jnp.concatenate(
        [
            first_half * cosine_table - second_half * sine_table,
            second_half * cosine_table + first_half * sine_table,
        ],
        axis=-1,
    )


def on_device(
    arrived,
    destination,
    query_of,
    lengths,
    attn_gain,
    q_weight,
    q_bias,
    k_weight,
    v_weight,
    v_bias,
    o_weight,
    mlp_gain,
    w_gate,
    w_up,
    w_down,
    final_gain,
    score_weight,
):
    group_index = lax.axis_index("dp")
    tensor_index = lax.axis_index(TENSOR)
    tensor_count = lax.axis_size(TENSOR)
    row_blocks = lax.all_to_all(arrived, TENSOR, split_axis=1, concat_axis=0, tiled=True)
    pairs_here = row_blocks.shape[0]
    row_targets = lax.dynamic_slice_in_dim(destination, group_index * pairs_here, pairs_here)
    local_order = jnp.argsort(row_targets * pairs_here + jnp.arange(pairs_here, dtype=jnp.int32))
    sorted_rows = jnp.transpose(jnp.take(row_blocks, local_order, axis=0), (1, 0, 2))
    resident = lax.all_to_all(sorted_rows, "dp", split_axis=1, concat_axis=1, tiled=True)
    total_pairs = destination.shape[0]
    global_order = jnp.argsort(destination * total_pairs + jnp.arange(total_pairs, dtype=jnp.int32))
    my_pairs = lax.dynamic_slice_in_dim(global_order, group_index * pairs_here, pairs_here)
    my_lengths = jnp.take(lengths, my_pairs)
    my_queries = jnp.take(query_of, my_pairs)
    seq_local = resident.shape[0]
    seq_len = seq_local * tensor_count
    heads_here = q_weight.shape[1] // HEAD_DIM
    kv_head = tensor_index * heads_here // (HEADS // KV_HEADS)
    key_cols = lax.dynamic_slice_in_dim(k_weight, kv_head * HEAD_DIM, HEAD_DIM, 1)
    value_cols = lax.dynamic_slice_in_dim(v_weight, kv_head * HEAD_DIM, HEAD_DIM, 1)
    value_shift = lax.dynamic_slice_in_dim(v_bias, kv_head * HEAD_DIM, HEAD_DIM)
    joint_weight = jnp.concatenate([q_weight, key_cols, value_cols], axis=1)
    joint_bias = jnp.concatenate(
        [
            q_bias.astype(jnp.float32),
            jnp.zeros((HEAD_DIM,), jnp.float32),
            value_shift.astype(jnp.float32),
        ]
    )
    frequencies = frequency_table(HEAD_DIM)
    query_width = heads_here * HEAD_DIM
    normed = rms_scale(resident, attn_gain).astype(jnp.bfloat16)
    piece_rows = lax.all_gather(normed, TENSOR, axis=0, tiled=True)
    row_total = piece_rows.shape[0]
    projected_rows = (
        jnp.einsum("spd,de->spe", piece_rows, joint_weight, preferred_element_type=jnp.float32)
        + joint_bias
    )
    angles = (
        jnp.arange(row_total, dtype=jnp.int32).astype(jnp.float32)[:, None] * frequencies[None, :]
    )
    cosine_table = jnp.cos(angles)[:, None, None, :]
    sine_table = jnp.sin(angles)[:, None, None, :]
    query_rows = projected_rows[..., :query_width].reshape(
        row_total, pairs_here, heads_here, HEAD_DIM
    )
    key_rows = projected_rows[..., query_width : query_width + HEAD_DIM].reshape(
        row_total, pairs_here, 1, HEAD_DIM
    )
    value_rows = projected_rows[..., query_width + HEAD_DIM :]
    query_rows = rotate(query_rows, cosine_table, sine_table).reshape(
        row_total, pairs_here, query_width
    )
    key_rows = rotate(key_rows, cosine_table, sine_table).reshape(row_total, pairs_here, HEAD_DIM)
    projected = jnp.concatenate([query_rows, key_rows, value_rows], axis=-1).astype(jnp.bfloat16)
    query_all = projected[..., :query_width].reshape(seq_len, pairs_here, heads_here, HEAD_DIM)
    key_all = projected[..., query_width : query_width + HEAD_DIM]
    value_all = projected[..., query_width + HEAD_DIM :]
    logits = jnp.einsum(
        "qphe,kpe->phqk", query_all, key_all, preferred_element_type=jnp.float32
    ) / math.sqrt(HEAD_DIM)
    positions = jnp.arange(seq_len, dtype=jnp.int32)
    allowed = (positions[None, :] <= positions[:, None])[None, :, :] & (
        positions[None, None, :] < my_lengths[:, None, None]
    )
    logits = jnp.where(allowed[:, None, :, :], logits, -1e30)
    shifted = jnp.exp(logits - jnp.max(logits, axis=-1, keepdims=True))
    probs = (shifted / jnp.sum(shifted, axis=-1, keepdims=True)).astype(jnp.bfloat16)
    context = jnp.einsum(
        "phqk,kpe->qphe", probs, value_all, preferred_element_type=jnp.float32
    ).astype(jnp.bfloat16)
    context = context.reshape(seq_len, pairs_here, query_width)
    own_context = lax.all_to_all(context, TENSOR, split_axis=0, concat_axis=2, tiled=True)
    attended = jnp.einsum(
        "spe,ed->spd",
        own_context,
        gather_axes(o_weight, TENSOR, 0),
        preferred_element_type=jnp.float32,
    )
    after_attention = (resident.astype(jnp.float32) + attended).astype(jnp.bfloat16)
    normed_mlp = rms_scale(after_attention, mlp_gain).astype(jnp.bfloat16)
    piece_rows = lax.all_gather(normed_mlp, TENSOR, axis=0, tiled=True)
    gate_values = jnp.einsum("spd,df->spf", piece_rows, w_gate, preferred_element_type=jnp.float32)
    up_values = jnp.einsum("spd,df->spf", piece_rows, w_up, preferred_element_type=jnp.float32)
    activated = (jax.nn.silu(gate_values) * up_values).astype(jnp.bfloat16)
    mlp_sum = lax.psum_scatter(
        jnp.einsum("spf,fd->spd", activated, w_down, preferred_element_type=jnp.float32).astype(
            jnp.bfloat16
        ),
        TENSOR,
        scatter_dimension=0,
        tiled=True,
    ).astype(jnp.float32)
    hidden_out = (after_attention.astype(jnp.float32) + mlp_sum).astype(jnp.bfloat16)
    local_positions = tensor_index * seq_local + jnp.arange(seq_local, dtype=jnp.int32)
    is_last = (local_positions[:, None] == (my_lengths - 1)[None, :]).astype(jnp.bfloat16)
    last_rows = jnp.einsum("sp,spd->pd", is_last, hidden_out, preferred_element_type=jnp.float32)
    partial_score = jnp.sum(rms_scale(last_rows, final_gain) * score_weight, axis=-1)
    pair_score = taken_together(partial_score, TENSOR)
    query_total = lax.axis_size("dp") * QUERY_DP
    membership = (my_queries[:, None] == jnp.arange(query_total, dtype=jnp.int32)[None, :]).astype(
        jnp.float32
    )
    totals = taken_together(jnp.dot(pair_score, membership), "dp")
    mean_all = totals / (total_pairs // query_total)
    centred = pair_score - jnp.dot(membership, mean_all)
    query_mean = lax.dynamic_slice_in_dim(mean_all, group_index * QUERY_DP, QUERY_DP)
    return (hidden_out, centred, query_mean)


def solution(mesh):
    split = Mesh(mesh.devices.reshape(mesh.shape["dp"], 4, 2), ("dp", "tensor_0", "tensor_1"))
    placed = (
        P(DP_TENSOR, None, None),
        P(),
        P(),
        P(),
        P(),
        P(None, TENSOR),
        P(TENSOR),
        P(),
        P(),
        P(),
        P(TENSOR, None),
        P(),
        P(None, TENSOR),
        P(None, TENSOR),
        P(TENSOR, None),
        P(),
        P(),
    )
    return jax.shard_map(
        on_device,
        mesh=split,
        in_specs=placed,
        out_specs=(P(TENSOR, "dp", None), P("dp"), P("dp")),
        check_vma=False,
    )
```

profile of v0, /device:TPU:1, one launch (start us, length us, event | category | flops | bytes accessed | tf_op | source)
XLA Modules:
  0.0 443.9 jit_solution(2030019210064797637)
XLA Ops:
  7.2 3.0 copy.56
  10.2 8.3 %all-to-all-start = ((bf16[2,128,1536]{2,0,1:T(2,128)(2,1)}), bf16[2,128,1536]{2,0,1:T(2,128)(2,1)}, u32[]{:S(2)}, u32[]{:S(2)}) async-start(bf16[2,128,1536]{2,0,1:T(2,128)(2,1)} %copy.56), calls=%async_computation | async-start | bytes 1572864 | tf_op jit(solution)/shard_map/all_to_all | solution.py:81
  18.5 0.8 iota_add_fusion.2
  19.3 1.2 sort.34
  20.5 0.7 iota_add_fusion
  21.2 3.2 sort.35
  24.5 7.3 %all-to-all-done = bf16[2,128,1536]{2,0,1:T(2,128)(2,1)} async-done(((bf16[2,128,1536]{2,0,1:T(2,128)(2,1)}), bf16[2,128,1536]{2,0,1:T(2,128)(2,1)}, u32[]{:S(2)}, u32[]{:S(2)}) %all-to-all-start) | async-done | bytes 786464 | tf_op jit(solution)/shard_map/all_to_all | solution.py:81
  31.8 1.2 copy.57
  33.0 0.9 copy.58
  34.0 2.6 gather_fusion
  36.6 1.3 select_bitcast_fusion
  37.9 19.4 %all_to_all.53 = bf16[16,16,1536]{2,0,1:T(8,128)(2,1)S(1)} all-to-all(bf16[16,16,1536]{2,0,1:T(8,128)(2,1)S(1)} %select_bitcast_fusion), channel_id=1, replica_groups=mesh['dp'=16,'tensor_0'=4,'tensor_1'=2] {'dp'}, dimensions={1} | all-to-all | bytes 1572864 | tf_op jit(solution)/shard_map/all_to_all | solution.py:86
  57.5 0.6 copy-done.3
  58.1 1.1 fusion.17
  59.3 13.9 %all_gather.13 = bf16[256,1536]{1,0:T(8,128)(2,1)} all-gather(bf16[128,1536]{1,0:T(8,128)(2,1)} %param.29), channel_id=1, replica_groups=mesh['dp'=16,'tensor_0'=4,'tensor_1'=2] {'tensor_1'}, dimensions={0}, use_global_device_ids=true | all-gather | bytes 1179648 | tf_op jit(solution)/shard_map/all_gather | solution.py:20
  73.4 0.7 gather_fusion.1
  74.0 0.7 gather_fusion.2
  74.9 0.9 multiply_cosine_fusion
  75.9 2.1 constant_dynamic-slice_fusion
  77.9 66.0 %all-gather.4.cloned.1.call-done = bf16[128,16,1536]{2,0,1:T(8,128)(2,1)} async-done(((bf16[16,16,1536]{2,0,1:T(8,128)(2,1)}), bf16[128,16,1536]{2,0,1:T(8,128)(2,1)}) %all-gather.4.cloned.1.call-update) | async-done | bytes 6291472 | tf_op jit(solution)/shard_map/all_gather | solution.py:110
  144.0 5.9 %convolution_add_fusion = f32[128,16,384]{2,0,1:T(8,128)S(1)} fusion(bf16[128,16,1536]{2,0,1:T(8,128)(2,1)} %all-gather.4.cloned.1.call-done, f32[384]{0:T(512)S(1)} %pad_maximum_fusion, bf16[1536,128]{1,0:T(8,128)(2,1)} %get-tuple-element.45, bf16[1536,128]{1,0:T(8,128)(2,1)} %get-tuple-element.46, bf16[1536,128]{1,0:T(8,128)(2,1)} %param.24), kind=kOutput, calls=%fused_computation.16 | convolution fusion | flops 2420244480 | bytes 10618368 | tf_op jit(solution)/shard_map/spd,de->spe/dot_general | solution.py:113
  149.8 0.3 slice_bitcast_fusion
  150.1 0.6 copy-done.6
  150.7 0.8 subtract_convert_fusion
  151.5 0.9 fusion.44
  152.5 1.2 fusion.20
  153.7 2.3 copy.61
  156.0 15.4 %all_to_all.54 = bf16[128,16,128]{2,1,0:T(8,128)(2,1)S(1)} all-to-all(bf16[128,16,128]{2,1,0:T(8,128)(2,1)} %copy.61), channel_id=1, replica_groups=mesh['dp'=16,'tensor_0'=4,'tensor_1'=2] {'tensor_0','tensor_1'}, dimensions={0} | all-to-all | bytes 1048576 | tf_op jit(solution)/shard_map/all_to_all | solution.py:150
  171.5 1.1 copy.73
  172.6 2.1 reshape.241
  174.7 14.6 %all-gather.6.cloned.1.call-done = bf16[1024,1536]{1,0:T(8,128)(2,1)} async-done(((bf16[256,1536]{1,0:T(8,128)(2,1)}), bf16[1024,1536]{1,0:T(8,128)(2,1)}) %all-gather.6.cloned.1.call-update) | async-done | bytes 3145744 | tf_op jit(solution)/shard_map/all_gather | solution.py:20
  189.3 3.3 multiply_reduce_fusion
  192.6 1.1 copy-done.5
  193.8 1.1 multiply_convert_fusion.1
  195.1 88.1 %all-gather.8.cloned.1.call-done = bf16[128,16,1536]{2,0,1:T(8,128)(2,1)} async-done(((bf16[16,16,1536]{2,0,1:T(8,128)(2,1)}), bf16[128,16,1536]{2,0,1:T(8,128)(2,1)}) %all-gather.8.cloned.1.call-update) | async-done | bytes 6291472 | tf_op jit(solution)/shard_map/all_gather | solution.py:159
  283.2 10.6 %fusion.1 = f32[128,16,1120]{0,2,1:T(8,128)S(1)} fusion(bf16[128,16,1536]{2,0,1:T(8,128)(2,1)} %all-gather.8.cloned.1.call-done, bf16[1536,1120]{0,1:T(8,128)(2,1)} %param.32), kind=kOutput, calls=%fused_computation.6 | convolution fusion | flops 7046430720 | bytes 18907136 | tf_op jit(solution)/shard_map/spd,df->spf/dot_general | solution.py:161
  293.9 8.7 %multiply_convert_fusion = bf16[128,16,1120]{0,2,1:T(8,128)(2,1)S(1)} fusion(f32[128,16,1120]{0,2,1:T(8,128)S(1)} %fusion.1, bf16[128,16,1536]{2,0,1:T(8,128)(2,1)S(1)} %copy-done.11, bf16[1536,1120]{0,1:T(8,128)(2,1)S(1)} %copy-done.12), kind=kOutput, calls=%fused_computation.3 | convolution fusion | flops 7060193280 | bytes 23494656 | tf_op jit(solution)/shard_map/spd,df->spf/dot_general | solution.py:160
  302.6 10.3 %convolution_convert_fusion = bf16[128,16,1536]{2,0,1:T(8,128)(2,1)} fusion(bf16[128,16,1120]{0,2,1:T(8,128)(2,1)S(1)} %multiply_convert_fusion, bf16[1120,1536]{1,0:T(8,128)(2,1)S(1)} %copy-done), kind=kOutput, calls=%fused_computation.4 | convolution fusion | flops 7049576448 | bytes 14319616 | tf_op jit(solution)/shard_map/spf,fd->spd/dot_general | solution.py:164
  313.1 95.8 %reduce-scatter.2.cloned.1.call-done = bf16[16,16,1536]{2,0,1:T(8,128)(2,1)} async-done(((bf16[128,16,1536]{2,0,1:T(8,128)(2,1)}), bf16[16,16,1536]{2,0,1:T(8,128)(2,1)}) %reduce-scatter.2.cloned.1.call-update) | async-done | bytes 786448 | tf_op jit(solution)/shard_map/reduce_scatter | solution.py:163
  408.9 1.8 add_convert_fusion
  410.7 0.9 copy-done.4
  412.2 8.9 %all_to_all.55 = f32[8,1,16]{2,1,0:T(1,128)S(1)} all-to-all(f32[8,1,16]{2,1,0:T(1,128)S(1)} %broadcast_in_dim.30), channel_id=1, replica_groups=mesh['dp'=16,'tensor_0'=4,'tensor_1'=2] {'tensor_0','tensor_1'}, dimensions={0} | all-to-all | bytes 1024 | tf_op jit(solution)/shard_map/all_to_all | solution.py:26
  421.3 0.6 broadcast_in_dim.31
  421.9 8.7 %all-to-all-start.4 = ((f32[16,1,32]{2,1,0:T(1,128)}), f32[16,1,32]{2,1,0:T(1,128)S(1)}, u32[]{:S(2)}, u32[]{:S(2)}) async-start(f32[16,1,32]{2,1,0:T(1,128)} %broadcast_in_dim.31), calls=%async_computation.5 | async-start | bytes 16384 | tf_op jit(solution)/shard_map/all_to_all | solution.py:26
  430.6 2.4 copy.66
  433.0 3.1 all-to-all-done.4
  436.1 0.7 fusion.25
  436.8 0.6 dynamic_slice.23
  (65 shorter events, 2.2 us)
Async XLA Ops:
  7.2 295.4 %copy-start = (bf16[1120,1536]{1,0:T(8,128)(2,1)S(1)}, bf16[1120,1536]{1,0:T(8,128)(2,1)}, u32[]{:S(2)}) copy-start(bf16[1120,1536]{1,0:T(8,128)(2,1)} %param.33) | copy-start | bytes 10321924
  10.2 21.7 %all-to-all-start = ((bf16[2,128,1536]{2,0,1:T(2,128)(2,1)}), bf16[2,128,1536]{2,0,1:T(2,128)(2,1)}, u32[]{:S(2)}, u32[]{:S(2)}) async-start(bf16[2,128,1536]{2,0,1:T(2,128)(2,1)} %copy.56), calls=%async_computation | async-start | bytes 1572864 | tf_op jit(solution)/shard_map/all_to_all | solution.py:81
  18.5 125.5 %all-gather.4.cloned.1.call-start = ((), (), s32[]{:S(2)}) async-start(), calls=%async_computation.6 | async-start | bytes 7077888 | tf_op jit(solution)/shard_map/all_gather | solution.py:110
  33.0 25.1 %copy-start.7 = (f32[1536]{0:T(1024)S(1)}, f32[1536]{0:T(1024)}, u32[]{:S(2)}) copy-start(f32[1536]{0:T(1024)} %param.23) | copy-start | bytes 18436
  37.9 35.5 %copy-start.13 = (bf16[128]{0:T(256)(128)(2,1)S(1)}, bf16[128]{0:T(256)(128)(2,1)}, u32[]{:S(2)}) copy-start(bf16[128]{0:T(256)(128)(2,1)} %param.25) | copy-start | bytes 772
  37.9 35.5 %copy-start.1 = (s32[256]{0:T(256)S(1)}, s32[256]{0:T(256)}, u32[]{:S(2)}) copy-start(s32[256]{0:T(256)} %param.22) | copy-start | bytes 3076
  37.9 36.2 %copy-start.2 = (s32[256]{0:T(256)S(1)}, s32[256]{0:T(256)}, u32[]{:S(2)}) copy-start(s32[256]{0:T(256)} %param.21) | copy-start | bytes 3076
  57.2 0.9 copy-start.3
  57.2 17.5 %copy-start.14 = (bf16[256]{0:T(256)(128)(2,1)S(1)}, bf16[256]{0:T(256)(128)(2,1)}, u32[]{:S(2)}) copy-start(bf16[256]{0:T(256)(128)(2,1)} %param.28) | copy-start | bytes 1540
  59.3 130.0 %all-gather.6.cloned.1.call-start = ((), (), s32[]{:S(2)}) async-start(), calls=%async_computation.7 | async-start | bytes 3932160 | tf_op jit(solution)/shard_map/all_gather | solution.py:20
  73.3 210.0 %all-gather.8.cloned.1.call-start = ((), (), s32[]{:S(2)}) async-start(), calls=%async_computation.8 | async-start | bytes 7077888 | tf_op jit(solution)/shard_map/all_gather | solution.py:159
  149.8 0.8 copy-start.6
  172.6 21.2 %copy-start.8 = (f32[1536]{0:T(1024)S(1)}, f32[1536]{0:T(1024)}, u32[]{:S(2)}) copy-start(f32[1536]{0:T(1024)} %param.30) | copy-start | bytes 18436
  192.6 1.1 copy-start.5
  194.9 214.0 %reduce-scatter.2.cloned.1.call-start = ((), (), s32[]{:S(2)}) async-start(), calls=%async_computation.9 | async-start | bytes 7077888 | tf_op jit(solution)/shard_map/reduce_scatter | solution.py:163
  283.2 10.6 %copy-start.11 = (bf16[128,16,1536]{2,0,1:T(8,128)(2,1)S(1)}, bf16[128,16,1536]{2,0,1:T(8,128)(2,1)}, u32[]{:S(2)}) copy-start(bf16[128,16,1536]{2,0,1:T(8,128)(2,1)} %all-gather.8.cloned.1.call-done) | copy-start | bytes 18874372
  283.2 10.6 %copy-start.12 = (bf16[1536,1120]{0,1:T(8,128)(2,1)S(1)}, bf16[1536,1120]{0,1:T(8,128)(2,1)}, u32[]{:S(2)}) copy-start(bf16[1536,1120]{0,1:T(8,128)(2,1)} %param.31) | copy-start | bytes 10321924
  312.9 99.1 %copy-start.9 = (f32[1536]{0:T(1024)S(1)}, f32[1536]{0:T(1024)}, u32[]{:S(2)}) copy-start(f32[1536]{0:T(1024)} %param.35) | copy-start | bytes 18436
  312.9 99.1 %copy-start.10 = (f32[1536]{0:T(1024)S(1)}, f32[1536]{0:T(1024)}, u32[]{:S(2)}) copy-start(f32[1536]{0:T(1024)} %param.34) | copy-start | bytes 18436
  410.7 0.9 copy-start.4
  421.9 14.2 %all-to-all-start.4 = ((f32[16,1,32]{2,1,0:T(1,128)}), f32[16,1,32]{2,1,0:T(1,128)S(1)}, u32[]{:S(2)}, u32[]{:S(2)}) async-start(f32[16,1,32]{2,1,0:T(1,128)} %broadcast_in_dim.31), calls=%async_computation.5 | async-start | bytes 16384 | tf_op jit(solution)/shard_map/all_to_all | solution.py:26
Sparse Core Ops, SparseCore 0:
  59.4 84.5 all-gather.3
  145.6 43.6 all-gather.5
  195.0 88.1 all-gather.7
  313.0 95.8 reduce-scatter.1
where the time goes:
time: 445 us; the launch traced here: 444 us
  waiting for transfers between devices  275 us (62%)
  blocking collectives  57.6 us (13%)
  matrix products  42 us (9%)
  local copies, waits for them, and re-layouts  23.9 us (5%)
  starting transfers between devices  17.3 us (4%)
  between operations  14.1 us (3%)
  other arithmetic  14 us (3%)
    reduce_scatter x1, waiting for transfers between devices, on_device(): lax.psum_scatter(jnp.einsum('spf,fd->spd', activated, w_down, preferred_e...  95.8 us
    all_gather x1, waiting for transfers between devices, on_device(): piece_rows = lax.all_gather(normed_mlp, TENSOR, axis=0, tiled=True)  88.1 us
    all_gather x1, waiting for transfers between devices, on_device(): piece_rows = lax.all_gather(normed, TENSOR, axis=0, tiled=True)  66 us
    all_to_all x1, blocking collectives, on_device(): lax.all_to_all(sorted_rows, 'dp', split_axis=1, concat_axis=1, tiled=True)  19.4 us
    all_to_all x1, blocking collectives, on_device(): lax.all_to_all(context, TENSOR, split_axis=0, concat_axis=2, tiled=True)  15.4 us
    all_gather x1, waiting for transfers between devices, gather_axes(): x = lax.all_gather(x, axis, axis=dim, tiled=True)  14.6 us
    all_gather x1, blocking collectives, gather_axes(): x = lax.all_gather(x, axis, axis=dim, tiled=True)  13.9 us
    dot_general x1, matrix products, on_device(): jnp.einsum('spd,df->spf', piece_rows, w_up, preferred_element_type=jnp.fl...  10.6 us
  transfers between devices with their start and end apart: 6, of which 6 were waited for; matrix products, arithmetic and copies ran while one was open for 6% of the time, Pallas kernels for 0%

commit v1 on v0

--- a/solution.py
+++ b/solution.py
@@ -13,6 +13,11 @@
 DP_TENSOR = ("dp", "tensor_0", "tensor_1")
 theta_base = 1000000.0
 norm_eps = 1e-06
+
+
+def gather_over(x, axis, dim):
+    sent = jnp.stack([x] * lax.axis_size(axis))
+    return jnp.concatenate(lax.all_to_all(sent, axis, 0, 0), axis=dim)
 
 
 def gather_axes(x, axes, dim):
@@ -156,7 +161,7 @@
     )
     after_attention = (resident.astype(jnp.float32) + attended).astype(jnp.bfloat16)
     normed_mlp = rms_scale(after_attention, mlp_gain).astype(jnp.bfloat16)
-    piece_rows = lax.all_gather(normed_mlp, TENSOR, axis=0, tiled=True)
+    piece_rows = gather_over(normed_mlp, TENSOR, 0)
     gate_values = jnp.einsum("spd,df->spf", piece_rows, w_gate, preferred_element_type=jnp.float32)
     up_values = jnp.einsum("spd,df->spf", piece_rows, w_up, preferred_element_type=jnp.float32)
     activated = (jax.nn.silu(gate_values) * up_values).astype(jnp.bfloat16)

time: 445 us -> 434 us (0.975)
  waiting for transfers between devices: 275 us -> 187 us
  blocking collectives: 57.6 us -> 135 us
    all_gather x1 -> x0, waiting for transfers between devices: 88.1 us -> none  [on_device(): piece_rows = lax.all_gather(normed_mlp, TENSOR, axis=0, tiled=True)]
    all_to_all x0 -> x1, blocking collectives: none -> 77.5 us  [gather_over(): return jnp.concatenate(lax.all_to_all(sent, axis, 0, 0), axis=dim)]
  transfers between devices with their start and end apart: 6 -> 5, of which waited for: 6 -> 5; matrix products, arithmetic and copies ran while one was open for 6% -> 6% of each run, Pallas kernels for 0% -> 0%
where the time goes in v1:
time: 434 us; the launch traced here: 433 us
  waiting for transfers between devices  187 us (43%)
  blocking collectives  135 us (31%)
  matrix products  40.8 us (9%)
  local copies, waits for them, and re-layouts  25.3 us (6%)
  starting transfers between devices  17.2 us (4%)
  between operations  14.1 us (3%)
  other arithmetic  13.1 us (3%)
    reduce_scatter x1, waiting for transfers between devices, on_device(): lax.psum_scatter(jnp.einsum('spf,fd->spd', activated, w_down, preferred_e...  96.3 us
    all_to_all x1, blocking collectives, gather_over(): return jnp.concatenate(lax.all_to_all(sent, axis, 0, 0), axis=dim)  77.5 us
    all_gather x1, waiting for transfers between devices, on_device(): piece_rows = lax.all_gather(normed, TENSOR, axis=0, tiled=True)  66 us
    all_to_all x1, blocking collectives, on_device(): lax.all_to_all(sorted_rows, 'dp', split_axis=1, concat_axis=1, tiled=True)  19.4 us
    all_to_all x1, blocking collectives, on_device(): lax.all_to_all(context, TENSOR, split_axis=0, concat_axis=2, tiled=True)  15.4 us
    all_gather x1, waiting for transfers between devices, gather_axes(): x = lax.all_gather(x, axis, axis=dim, tiled=True)  14.6 us
    all_gather x1, blocking collectives, gather_axes(): x = lax.all_gather(x, axis, axis=dim, tiled=True)  13.9 us
    dot_general x1, matrix products, on_device(): jnp.einsum('spf,fd->spd', activated, w_down, preferred_element_type=jnp.f...  10.3 us
  transfers between devices with their start and end apart: 5, of which 5 were waited for; matrix products, arithmetic and copies ran while one was open for 6% of the time, Pallas kernels for 0%

profile of v1, /device:TPU:1, one launch (start us, length us, event | category | flops | bytes accessed | tf_op | source)
XLA Modules:
  0.0 433.0 jit_solution(16589497834801438303)
XLA Ops:
  7.2 3.0 copy.58
  10.2 8.3 %all-to-all-start = ((bf16[2,128,1536]{2,0,1:T(2,128)(2,1)}), bf16[2,128,1536]{2,0,1:T(2,128)(2,1)}, u32[]{:S(2)}, u32[]{:S(2)}) async-start(bf16[2,128,1536]{2,0,1:T(2,128)(2,1)} %copy.58), calls=%async_computation | async-start | bytes 1572864 | tf_op jit(solution)/shard_map/all_to_all | solution.py:86
  18.5 0.8 iota_add_fusion.2
  19.3 1.2 sort.34
  20.5 0.7 iota_add_fusion
  21.2 3.2 sort.35
  24.5 7.3 %all-to-all-done = bf16[2,128,1536]{2,0,1:T(2,128)(2,1)} async-done(((bf16[2,128,1536]{2,0,1:T(2,128)(2,1)}), bf16[2,128,1536]{2,0,1:T(2,128)(2,1)}, u32[]{:S(2)}, u32[]{:S(2)}) %all-to-all-start) | async-done | bytes 786464 | tf_op jit(solution)/shard_map/all_to_all | solution.py:86
  31.8 1.2 copy.59
  33.0 0.9 copy.60
  34.0 2.6 gather_fusion
  36.6 1.3 select_bitcast_fusion
  37.9 19.4 %all_to_all.58 = bf16[16,16,1536]{2,0,1:T(8,128)(2,1)S(1)} all-to-all(bf16[16,16,1536]{2,0,1:T(8,128)(2,1)S(1)} %select_bitcast_fusion), channel_id=1, replica_groups=mesh['dp'=16,'tensor_0'=4,'tensor_1'=2] {'dp'}, dimensions={1} | all-to-all | bytes 1572864 | tf_op jit(solution)/shard_map/all_to_all | solution.py:91
  57.5 0.6 copy-done.3
  58.1 1.1 fusion.17
  59.3 13.9 %all_gather.10 = bf16[256,1536]{1,0:T(8,128)(2,1)} all-gather(bf16[128,1536]{1,0:T(8,128)(2,1)} %param.29), channel_id=1, replica_groups=mesh['dp'=16,'tensor_0'=4,'tensor_1'=2] {'tensor_1'}, dimensions={0}, use_global_device_ids=true | all-gather | bytes 1179648 | tf_op jit(solution)/shard_map/all_gather | solution.py:25
  73.4 0.7 gather_fusion.1
  74.0 0.7 gather_fusion.2
  74.9 0.9 multiply_cosine_fusion
  75.9 2.1 constant_dynamic-slice_fusion
  77.9 66.0 %all-gather.3.cloned.1.call-done = bf16[128,16,1536]{2,0,1:T(8,128)(2,1)} async-done(((bf16[16,16,1536]{2,0,1:T(8,128)(2,1)}), bf16[128,16,1536]{2,0,1:T(8,128)(2,1)}) %all-gather.3.cloned.1.call-update) | async-done | bytes 6291472 | tf_op jit(solution)/shard_map/all_gather | solution.py:115
  144.0 5.9 %convolution_add_fusion = f32[128,16,384]{2,0,1:T(8,128)S(1)} fusion(bf16[128,16,1536]{2,0,1:T(8,128)(2,1)} %all-gather.3.cloned.1.call-done, f32[384]{0:T(512)S(1)} %pad_maximum_fusion, bf16[1536,128]{1,0:T(8,128)(2,1)} %get-tuple-element.45, bf16[1536,128]{1,0:T(8,128)(2,1)} %get-tuple-element.46, bf16[1536,128]{1,0:T(8,128)(2,1)} %param.24), kind=kOutput, calls=%fused_computation.16 | convolution fusion | flops 2420244480 | bytes 10618368 | tf_op jit(solution)/shard_map/spd,de->spe/dot_general | solution.py:118
  150.1 0.6 copy-done.6
  150.7 0.8 subtract_convert_fusion
  151.5 0.9 fusion.44
  152.5 1.2 fusion.20
  153.7 2.3 copy.63
  156.0 15.4 %all_to_all.59 = bf16[128,16,128]{2,1,0:T(8,128)(2,1)S(1)} all-to-all(bf16[128,16,128]{2,1,0:T(8,128)(2,1)} %copy.63), channel_id=1, replica_groups=mesh['dp'=16,'tensor_0'=4,'tensor_1'=2] {'tensor_0','tensor_1'}, dimensions={0} | all-to-all | bytes 1048576 | tf_op jit(solution)/shard_map/all_to_all | solution.py:155
  171.5 1.1 copy.76
  172.6 2.1 reshape.247
  174.7 14.6 %all-gather.5.cloned.1.call-done = bf16[1024,1536]{1,0:T(8,128)(2,1)} async-done(((bf16[256,1536]{1,0:T(8,128)(2,1)}), bf16[1024,1536]{1,0:T(8,128)(2,1)}) %all-gather.5.cloned.1.call-update) | async-done | bytes 3145744 | tf_op jit(solution)/shard_map/all_gather | solution.py:25
  189.3 3.3 multiply_reduce_fusion
  192.6 1.1 copy-done.5
  194.0 0.8 stack.2
  194.7 77.5 %all_to_all.60 = bf16[8,16,16,1536]{3,1,2,0:T(8,128)(2,1)S(1)} all-to-all(bf16[8,16,16,1536]{3,1,2,0:T(8,128)(2,1)S(1)} %stack.2), channel_id=1, replica_groups=mesh['dp'=16,'tensor_0'=4,'tensor_1'=2] {'tensor_0','tensor_1'}, dimensions={0} | all-to-all | bytes 12582912 | tf_op jit(solution)/shard_map/all_to_all | solution.py:20
  272.2 0.6 copy.66
  272.9 9.5 %fusion.1 = f32[128,16,1120]{0,2,1:T(8,128)S(1)} fusion(bf16[128,16,1536]{2,0,1:T(8,128)(2,1)S(1)} %bitcast.109, bf16[1536,1120]{0,1:T(8,128)(2,1)} %param.32), kind=kOutput, calls=%fused_computation.6 | convolution fusion | flops 7046430720 | bytes 18907136 | tf_op jit(solution)/shard_map/spd,df->spf/dot_general | solution.py:166
  282.3 8.7 %multiply_convert_fusion = bf16[128,16,1120]{0,2,1:T(8,128)(2,1)S(1)} fusion(f32[128,16,1120]{0,2,1:T(8,128)S(1)} %fusion.1, bf16[128,16,1536]{2,0,1:T(8,128)(2,1)S(1)} %bitcast.110, bf16[1536,1120]{0,1:T(8,128)(2,1)S(1)} %copy-done.11), kind=kOutput, calls=%fused_computation.3 | convolution fusion | flops 7060193280 | bytes 23494656 | tf_op jit(solution)/shard_map/spd,df->spf/dot_general | solution.py:165
  291.1 10.3 %convolution_convert_fusion = bf16[128,16,1536]{2,0,1:T(8,128)(2,1)} fusion(bf16[128,16,1120]{0,2,1:T(8,128)(2,1)S(1)} %multiply_convert_fusion, bf16[1120,1536]{1,0:T(8,128)(2,1)S(1)} %copy-done), kind=kOutput, calls=%fused_computation.4 | convolution fusion | flops 7049576448 | bytes 14319616 | tf_op jit(solution)/shard_map/spf,fd->spd/dot_general | solution.py:169
  301.6 96.3 %reduce-scatter.2.cloned.1.call-done = bf16[16,16,1536]{2,0,1:T(8,128)(2,1)} async-done(((bf16[128,16,1536]{2,0,1:T(8,128)(2,1)}), bf16[16,16,1536]{2,0,1:T(8,128)(2,1)}) %reduce-scatter.2.cloned.1.call-update) | async-done | bytes 786448 | tf_op jit(solution)/shard_map/reduce_scatter | solution.py:168
  397.9 1.8 add_convert_fusion
  399.7 0.9 copy-done.4
  401.2 8.9 %all_to_all.61 = f32[8,1,16]{2,1,0:T(1,128)S(1)} all-to-all(f32[8,1,16]{2,1,0:T(1,128)S(1)} %broadcast_in_dim.30), channel_id=1, replica_groups=mesh['dp'=16,'tensor_0'=4,'tensor_1'=2] {'tensor_0','tensor_1'}, dimensions={0} | all-to-all | bytes 1024 | tf_op jit(solution)/shard_map/all_to_all | solution.py:31
  410.3 0.6 broadcast_in_dim.31
  410.9 8.7 %all-to-all-start.5 = ((f32[16,1,32]{2,1,0:T(1,128)}), f32[16,1,32]{2,1,0:T(1,128)S(1)}, u32[]{:S(2)}, u32[]{:S(2)}) async-start(f32[16,1,32]{2,1,0:T(1,128)} %broadcast_in_dim.31), calls=%async_computation.6 | async-start | bytes 16384 | tf_op jit(solution)/shard_map/all_to_all | solution.py:31
  419.7 2.4 copy.69
  422.1 3.1 all-to-all-done.5
  425.2 0.7 fusion.25
  425.9 0.6 dynamic_slice.23
  (63 shorter events, 2.4 us)
Async XLA Ops:
  7.2 283.9 %copy-start = (bf16[1120,1536]{1,0:T(8,128)(2,1)S(1)}, bf16[1120,1536]{1,0:T(8,128)(2,1)}, u32[]{:S(2)}) copy-start(bf16[1120,1536]{1,0:T(8,128)(2,1)} %param.33) | copy-start | bytes 10321924
  10.2 21.7 %all-to-all-start = ((bf16[2,128,1536]{2,0,1:T(2,128)(2,1)}), bf16[2,128,1536]{2,0,1:T(2,128)(2,1)}, u32[]{:S(2)}, u32[]{:S(2)}) async-start(bf16[2,128,1536]{2,0,1:T(2,128)(2,1)} %copy.58), calls=%async_computation | async-start | bytes 1572864 | tf_op jit(solution)/shard_map/all_to_all | solution.py:86
  18.5 125.5 %all-gather.3.cloned.1.call-start = ((), (), s32[]{:S(2)}) async-start(), calls=%async_computation.7 | async-start | bytes 7077888 | tf_op jit(solution)/shard_map/all_gather | solution.py:115
  33.0 25.1 %copy-start.7 = (f32[1536]{0:T(1024)S(1)}, f32[1536]{0:T(1024)}, u32[]{:S(2)}) copy-start(f32[1536]{0:T(1024)} %param.23) | copy-start | bytes 18436
  37.9 35.5 %copy-start.12 = (bf16[128]{0:T(256)(128)(2,1)S(1)}, bf16[128]{0:T(256)(128)(2,1)}, u32[]{:S(2)}) copy-start(bf16[128]{0:T(256)(128)(2,1)} %param.25) | copy-start | bytes 772
  37.9 35.5 %copy-start.1 = (s32[256]{0:T(256)S(1)}, s32[256]{0:T(256)}, u32[]{:S(2)}) copy-start(s32[256]{0:T(256)} %param.22) | copy-start | bytes 3076
  37.9 36.2 %copy-start.2 = (s32[256]{0:T(256)S(1)}, s32[256]{0:T(256)}, u32[]{:S(2)}) copy-start(s32[256]{0:T(256)} %param.21) | copy-start | bytes 3076
  57.2 0.9 copy-start.3
  57.2 17.5 %copy-start.13 = (bf16[256]{0:T(256)(128)(2,1)S(1)}, bf16[256]{0:T(256)(128)(2,1)}, u32[]{:S(2)}) copy-start(bf16[256]{0:T(256)(128)(2,1)} %param.28) | copy-start | bytes 1540
  59.3 130.0 %all-gather.5.cloned.1.call-start = ((), (), s32[]{:S(2)}) async-start(), calls=%async_computation.8 | async-start | bytes 3932160 | tf_op jit(solution)/shard_map/all_gather | solution.py:25
  73.3 324.7 %reduce-scatter.2.cloned.1.call-start = ((), (), s32[]{:S(2)}) async-start(), calls=%async_computation.9 | async-start | bytes 7077888 | tf_op jit(solution)/shard_map/reduce_scatter | solution.py:168
  149.8 0.8 copy-start.6
  172.6 21.2 %copy-start.8 = (f32[1536]{0:T(1024)S(1)}, f32[1536]{0:T(1024)}, u32[]{:S(2)}) copy-start(f32[1536]{0:T(1024)} %param.30) | copy-start | bytes 18436
  192.6 1.1 copy-start.5
  272.9 9.5 %copy-start.11 = (bf16[1536,1120]{0,1:T(8,128)(2,1)S(1)}, bf16[1536,1120]{0,1:T(8,128)(2,1)}, u32[]{:S(2)}) copy-start(bf16[1536,1120]{0,1:T(8,128)(2,1)} %param.31) | copy-start | bytes 10321924
  301.4 99.6 %copy-start.9 = (f32[1536]{0:T(1024)S(1)}, f32[1536]{0:T(1024)}, u32[]{:S(2)}) copy-start(f32[1536]{0:T(1024)} %param.35) | copy-start | bytes 18436
  301.4 99.6 %copy-start.10 = (f32[1536]{0:T(1024)S(1)}, f32[1536]{0:T(1024)}, u32[]{:S(2)}) copy-start(f32[1536]{0:T(1024)} %param.34) | copy-start | bytes 18436
  399.7 0.9 copy-start.4
  410.9 14.3 %all-to-all-start.5 = ((f32[16,1,32]{2,1,0:T(1,128)}), f32[16,1,32]{2,1,0:T(1,128)S(1)}, u32[]{:S(2)}, u32[]{:S(2)}) async-start(f32[16,1,32]{2,1,0:T(1,128)} %broadcast_in_dim.31), calls=%async_computation.6 | async-start | bytes 16384 | tf_op jit(solution)/shard_map/all_to_all | solution.py:31
Sparse Core Ops, SparseCore 0:
  59.4 84.5 all-gather.2
  145.6 43.6 all-gather.4
  301.5 96.3 reduce-scatter.1
